TPU v7x, 32 devices: a whole 2x2x4 slice. The times are simulated.
32 devices in a mesh: gx: 4 (over x, core), gy: 8 (over z, y).
Axes of the slice: x: 2, y: 2, z: 4, core: 2. Of those that a mesh axis runs over, the one named last changes fastest.
Arguments:
- log_crit: float32 [512, 512, 128], P('gx', 'gy'), may hold values from -4 to 4
- col_bins: int32 [512, 512, 4], P('gx', 'gy'), may hold values from 0 to 127
- rate_table: bfloat16 [128, 64], replicated, may hold values from 0.0039978027 to 0.059814453
- tile_mask: int32 [16, 16, 4], P('gx', 'gy'), may hold values from 0 to 1, as said below
- tile_route: int32 [16, 16, 4], P('gx', 'gy'), may hold values from 0 to 7, as said below
- filt_x: float32 [512], replicated, may hold values from 0.1 to 1, as said below
- filt_y: float32 [512], replicated, may hold values from 0.1 to 1, as said below
Outputs:
- recomb: float32 [512, 512, 128], P('gx', 'gy')
- smoothed: float32 [512, 512, 128], P('gx', 'gy')
- load: float32 [4, 8], P('gx', 'gy')
Inputs may be any that keep to these rules, and one draw needn't show every extreme that they name: `tile_mask`: tiles form blocks of 4 x 2 x 4 (indices a // 4, b // 2); among the blocks with the same a // 4, some block has all 32 tiles active. `tile_route`: counting only tiles with tile_mask 1: among the blocks with the same a // 4 at most 16 active tiles share a route, and in every draw some such row of blocks gives every route exactly 16; at most 4 active tiles of one block share a route, and in every draw some block has 4 that do. filt_x[m] == filt_x[512 - m] for 0 < m < 512. filt_y[n] == filt_y[512 - n] for 0 < n < 512.
All inputs are finite; a program needn't handle non-finite values.
Results may differ from a plain program's by a relative error of at most 0.0003.
Values sent between devices are 32-bit elements; how exact they have to be, the bound alone decides.
A program may use at most 128 MiB of HBM per device.

v0:
```python
import math

import jax
import jax.numpy as jnp
from jax import lax
from jax.sharding import PartitionSpec as P

steepness = 3.0


def evaluate(field_rows, bin_rows, rate_table):
    tile_count, tile_cells = field_rows.shape
    columns = bin_rows.shape[1]
    z_depth = tile_cells // columns
    bins_total, nodes_total = rate_table.shape
    node_grid = -2.5 + 5.0 * jnp.arange(nodes_total, dtype=jnp.float32) / (nodes_total - 1)
    levels = jnp.arange(bins_total, dtype=jnp.int32)

    def pair_value(operands):
        pair_field, pair_bins = operands
        onehot = (pair_bins.reshape(-1)[:, None] == levels[None, :]).astype(jnp.bfloat16)
        table_rows = jnp.dot(onehot, rate_table, preferred_element_type=jnp.float32).reshape(
            2, columns, 1, nodes_total
        )
        cutoff = jax.nn.sigmoid(
            (pair_field.reshape(2, columns, z_depth, 1) - node_grid) * steepness
        )
        return jnp.sum(cutoff * table_rows, axis=-1).reshape(2, tile_cells)

    values = lax.map(
        pair_value,
        (
            field_rows.reshape(tile_count // 2, 2, tile_cells),
            bin_rows.reshape(tile_count // 2, 2, columns),
        ),
    )
    return values.reshape(tile_count, tile_cells)


def dft_table(length, gain):
    half = length // 2
    indices = jnp.arange(length, dtype=jnp.int32)
    freq = jnp.concatenate(
        [jnp.arange(half + 1, dtype=jnp.int32), jnp.arange(1, half, dtype=jnp.int32)]
    )
    angles = (
        2.0 * math.pi / length * (indices[:, None] * freq[None, :] % length).astype(jnp.float32)
    )
    is_cosine = indices[None, :] < half + 1
    table = jnp.where(is_cosine, jnp.cos(angles), jnp.sin(angles))
    weight = jnp.concatenate([gain[: half + 1], gain[1:half]])
    doubled = jnp.where((freq == 0) | (freq == half), 1.0, 2.0).astype(jnp.float32)
    return (table, weight * doubled / length)


def smooth_plane(pencil, filt_x, filt_y):
    z_local, size_x, size_y = pencil.shape
    table_y, weight_y = dft_table(size_y, filt_y)
    spectrum = (
        jnp.dot(pencil.reshape(-1, size_y), table_y, precision=lax.Precision.HIGHEST) * weight_y
    )
    along_y = jnp.dot(spectrum, table_y.T, precision=lax.Precision.HIGHEST).reshape(
        z_local, size_x, size_y
    )
    table_x, weight_x = dft_table(size_x, filt_x)
    spectrum_x = (
        jnp.einsum("zxy,xk->zky", along_y, table_x, precision=lax.Precision.HIGHEST)
        * weight_x[None, :, None]
    )
    return jnp.einsum("zky,xk->zxy", spectrum_x, table_x, precision=lax.Precision.HIGHEST)


def on_device(log_crit, col_bins, rate_table, tile_mask, tile_route, filt_x, filt_y):
    blocks_x, blocks_y, blocks_z = tile_mask.shape
    cells_x, cells_y, depth_all = log_crit.shape
    tile_edge = cells_x // blocks_x
    tile_count = blocks_x * blocks_y * blocks_z
    tile_cells = tile_edge * tile_edge * tile_edge
    tile_data = (
        log_crit.reshape(blocks_x, tile_edge, blocks_y, tile_edge, blocks_z, tile_edge)
        .transpose(0, 2, 4, 1, 3, 5)
        .reshape(tile_count, tile_cells)
    )
    tile_bins = (
        col_bins.reshape(blocks_x, tile_edge, blocks_y, tile_edge, blocks_z)
        .transpose(0, 2, 4, 1, 3)
        .reshape(tile_count, tile_edge * tile_edge)
    )
    is_active = tile_mask.reshape(tile_count)
    target = tile_route.reshape(tile_count)
    receivers = lax.axis_size("gy")
    span_x = lax.axis_size("gx")
    capacity = tile_count // 2
    recomb_tiles = evaluate(tile_data, tile_bins, rate_table)
    recomb_tiles = jnp.where(is_active[:, None] == 1, recomb_tiles, 0.0)
    tile_means = jnp.mean(recomb_tiles, axis=1)
    route_ids = jnp.arange(receivers, dtype=jnp.int32)
    contribution = (
        jnp.sum(jnp.where(target[:, None] == route_ids[None, :], tile_means[:, None], 0.0), axis=0)
        / capacity
    )
    device_load = lax.psum_scatter(contribution, "gy", scatter_dimension=0, tiled=True)[0]
    recomb = (
        recomb_tiles.reshape(blocks_x, blocks_y, blocks_z, tile_edge, tile_edge, tile_edge)
        .transpose(0, 3, 1, 4, 2, 5)
        .reshape(cells_x, cells_y, depth_all)
    )
    z_first = recomb.transpose(2, 0, 1)
    pencil = lax.all_to_all(
        lax.all_to_all(z_first, "gx", split_axis=0, concat_axis=1, tiled=True),
        "gy",
        split_axis=0,
        concat_axis=2,
        tiled=True,
    )
    smoothed_pencil = smooth_plane(pencil, filt_x, filt_y)
    returned_pencil = lax.all_to_all(
        lax.all_to_all(smoothed_pencil, "gx", split_axis=1, concat_axis=0, tiled=True),
        "gy",
        split_axis=2,
        concat_axis=0,
        tiled=True,
    )
    z_local = depth_all // (span_x * receivers)
    smoothed = (
        returned_pencil.reshape(receivers, span_x, z_local, cells_x, cells_y)
        .transpose(3, 4, 1, 0, 2)
        .reshape(cells_x, cells_y, depth_all)
    )
    return (recomb, smoothed, device_load.reshape(1, 1))


def solution(mesh):
    placed = (
        P("gx", "gy", None),
        P("gx", "gy", None),
        P(),
        P("gx", "gy", None),
        P("gx", "gy", None),
        P(),
        P(),
    )
    return jax.shard_map(
        on_device,
        mesh=mesh,
        in_specs=placed,
        out_specs=(P("gx", "gy", None), P("gx", "gy", None), P("gx", "gy")),
        check_vma=False,
    )
```

profile of v0, /device:TPU:8, one launch (start us, length us, event | category | flops | bytes accessed | tf_op | source)
XLA Modules:
  0.0 667.1 jit_solution(11711818687086749989)
XLA Ops:
  0.6 12.9 %reshape.155 = f32[4,32,2,32,4,32]{5,4,3,2,1,0:T(4,128)} reshape(f32[128,64,128]{2,1,0:T(8,128)} %param.9) | data formatting | bytes 8388608 | tf_op jit(solution)/shard_map/reshape | solution.py:80
  13.6 12.6 %copy.91 = f32[4,32,2,32,4,32]{5,3,1,4,2,0:T(8,128)} copy(f32[4,32,2,32,4,32]{5,4,3,2,1,0:T(4,128)} %reshape.155) | data formatting | bytes 8388608 | tf_op jit(solution)/shard_map/reshape | solution.py:80
  26.2 16.7 %reshape_reshape.6 = f32[16,2,32768]{2,1,0:T(2,128)} reshape(f32[4,2,4,32,32,32]{5,4,3,2,1,0:T(8,128)} %bitcast.85) | data formatting | bytes 8388608 | tf_op jit(solution)/shard_map/reshape;reshape | solution.py:33
  43.8 162.5 %while.12 = (s32[]{:T(128)}, f32[16,2,32768]{2,1,0:T(2,128)}, f32[16,2,32768]{2,1,0:T(2,128)}, s32[16,2,1024]{2,1,0:T(2,128)S(1)}, bf16[128,64]{0,1:T(8,128)(2,1)S(1)}) while((s32[]{:T(128)}, f32[16,2,32768]{2,1,0:T(2,128)}, f32[16,2,32768]{2,1,0:T(2,128)}, s32[16,2,1024]{2,1,0:T(2,128)S(1)}, ...), condition=%wide.region_2.3_spmd.clone.clone, body=%wide.region_0.2_spmd.clone.sunk.clone | while | flops 63111296 | bytes 5825105 | solution.py:30
  46.4 6.0 multiply_reduce_fusion.3
  56.5 6.0 multiply_reduce_fusion.3
  76.8 6.0 multiply_reduce_fusion.3
  97.1 6.0 multiply_reduce_fusion.3
  107.3 6.0 multiply_reduce_fusion.3
  117.5 6.0 multiply_reduce_fusion.3
  127.6 6.0 multiply_reduce_fusion.3
  137.8 6.0 multiply_reduce_fusion.3
  147.9 6.0 multiply_reduce_fusion.3
  158.1 6.0 multiply_reduce_fusion.3
  168.2 6.0 multiply_reduce_fusion.3
  178.4 6.0 multiply_reduce_fusion.3
  188.6 6.0 multiply_reduce_fusion.3
  198.7 6.0 multiply_reduce_fusion.3
  206.3 15.3 %reshape.157 = f32[4,2,4,32,32,32]{5,4,3,2,1,0:T(8,128)} reshape(f32[16,2,32768]{2,1,0:T(2,128)} %get-tuple-element.40) | data formatting | bytes 8388608 | tf_op jit(solution)/shard_map/reshape | solution.py:37
  221.6 21.9 %copy.65 = f32[4,2,4,32,32,32]{3,0,4,1,5,2:T(4,128)} copy(f32[4,2,4,32,32,32]{5,4,3,2,1,0:T(8,128)} %reshape.157) | data formatting | bytes 8388608 | tf_op jit(solution)/shard_map/reshape | solution.py:37
  243.7 16.4 %select_bitcast_fusion = f32[4,32,2,32,4,32]{1,0,3,2,5,4:T(4,128)} fusion(f32[4,2,4,32,32,32]{3,0,4,1,5,2:T(4,128)} %copy.65, pred[4,2,4]{0,1,2:T(4,128)(4,1)S(1)} %copy.62), kind=kLoop, calls=%fused_computation.13 | loop fusion | flops 1048576 | bytes 8388640 | tf_op jit(solution)/shard_map/transpose | solution.py:105
  260.1 13.5 %reshape.158 = f32[128,64,128]{0,1,2:T(8,128)} reshape(f32[4,32,2,32,4,32]{1,0,3,2,5,4:T(4,128)} %select_bitcast_fusion) | data formatting | bytes 8388608 | tf_op jit(solution)/shard_map/reshape | solution.py:106
  273.5 51.9 %all_to_all.66 = f32[128,128,64]{1,2,0:T(8,128)S(1)} all-to-all(f32[128,128,64]{1,2,0:T(8,128)} %bitcast.87), channel_id=1, replica_groups=mesh['gx'=4,'gy'=8] {'gx'}, dimensions={0} | all-to-all | bytes 8388608 | tf_op jit(solution)/shard_map/all_to_all | solution.py:110
  328.0 6.6 all-to-all-start.1
  335.0 89.8 %all-to-all-done.1 = f32[32,512,64]{1,2,0:T(8,128)} async-done(((f32[32,512,64]{1,2,0:T(8,128)}), f32[32,512,64]{1,2,0:T(8,128)}, u32[]{:S(2)}, u32[]{:S(2)}) %all-to-all-start.1) | async-done | bytes 4194336 | tf_op jit(solution)/shard_map/all_to_all | solution.py:109
  431.6 11.4 %fusion.25 = f32[2048,512]{1,0:T(8,128)S(1)} fusion(f32[2048,512]{0,1:T(8,128)S(1)} %bitcast.88, s32[512]{0:T(512)S(1)} %get-tuple-element.78, pred[512]{0:T(512)(128)(4,1)S(1)} %iota_compare_fusion.3), kind=kOutput, calls=%fused_computation.37 | convolution fusion | flops 6446383104 | bytes 8391168 | tf_op jit(solution)/shard_map/dot_general | solution.py:60
  443.0 11.2 %fusion.9 = f32[2048,512]{1,0:T(8,128)S(1)} fusion(f32[2048,512]{1,0:T(8,128)S(1)} %fusion.25, f32[512]{0:T(512)S(1)} %fusion.26, s32[512]{0:T(512)S(1)} %get-tuple-element.78, pred[512]{0:T(512)(128)(4,1)S(1)} %iota_compare_fusion.3), kind=kOutput, calls=%fused_computation.19 | convolution fusion | flops 6447431680 | bytes 8393216 | tf_op jit(solution)/shard_map/dot_general | solution.py:62
  454.2 11.8 %fusion.19 = f32[512,4,512]{2,0,1:T(8,128)S(1)} fusion(f32[4,512,512]{2,1,0:T(8,128)S(1)} %bitcast.97, s32[512]{0:T(512)S(1)} %get-tuple-element.78, pred[512]{0:T(512)(128)(4,1)S(1)} %iota_compare_fusion.3), kind=kOutput, calls=%fused_computation.30 | convolution fusion | flops 6446383104 | bytes 8391168 | tf_op jit(solution)/shard_map/zxy,xk->zky/dot_general | solution.py:67
  466.0 11.8 %fusion.11 = f32[4,512,512]{2,1,0:T(8,128)S(1)} fusion(f32[512,4,512]{2,0,1:T(8,128)S(1)} %fusion.19, f32[512]{0:T(512)S(1)} %get-tuple-element.76, s32[512]{0:T(512)S(1)} %get-tuple-element.78, pred[512]{0:T(512)(128)(4,1)S(1)} %iota_compare_fusion.3), kind=kOutput, calls=%fused_computation.21 | convolution fusion | flops 6447431680 | bytes 8393216 | tf_op jit(solution)/shard_map/zky,xk->zxy/dot_general | solution.py:70
  480.5 50.7 %all_to_all.67 = f32[4,512,512]{2,0,1:T(4,128)S(1)} all-to-all(f32[4,512,512]{2,0,1:T(4,128)S(1)} %copy.69), channel_id=1, replica_groups=mesh['gx'=4,'gy'=8] {'gx'}, dimensions={1} | all-to-all | bytes 8388608 | tf_op jit(solution)/shard_map/all_to_all | solution.py:118
  540.7 7.0 %all-to-all-start.3 = ((f32[16,128,512]{1,0,2:T(8,128)}), f32[16,128,512]{1,0,2:T(8,128)}, u32[]{:S(2)}, u32[]{:S(2)}) async-start(f32[16,128,512]{1,0,2:T(8,128)} %copy.72), calls=%async_computation.3 | async-start | bytes 8388608 | tf_op jit(solution)/shard_map/all_to_all | solution.py:117
  552.2 96.5 %all-reduce = f32[8]{0:T(128)S(1)} all-reduce(f32[8]{0:T(128)S(1)} %broadcast_multiply_fusion.1), channel_id=2, replica_groups=mesh['gx'=4,'gy'=8] {'gy'}, use_global_device_ids=true, to_apply=%region_5.6.clone | all-reduce | flops 8 | bytes 64
  (226 shorter events, 124.0 us)
Async XLA Ops:
  26.2 16.7 %copy-start.1 = (s32[128,64,4]{0,2,1:T(4,128)S(1)}, s32[128,64,4]{0,2,1:T(4,128)}, u32[]{:S(2)}) copy-start(s32[128,64,4]{0,2,1:T(4,128)} %param.10) | copy-start | bytes 393220
  26.2 17.6 %copy-start = (bf16[128,64]{0,1:T(8,128)(2,1)S(1)}, bf16[128,64]{0,1:T(8,128)(2,1)}, u32[]{:S(2)}) copy-start(bf16[128,64]{0,1:T(8,128)(2,1)} %param.11) | copy-start | bytes 49156
  221.6 21.9 %copy-start.4 = (s32[4,2,4]{2,1,0:T(2,128)S(1)}, s32[4,2,4]{2,1,0:T(2,128)}, u32[]{:S(2)}) copy-start(s32[4,2,4]{2,1,0:T(2,128)} %param.12) | copy-start | bytes 388
  328.0 6.7 copy-start.2
  328.0 6.7 %copy-start.3 = (f32[512]{0:T(512)S(1)}, f32[512]{0:T(512)}, u32[]{:S(2)}) copy-start(f32[512]{0:T(512)} %param.15) | copy-start | bytes 6148
  328.0 96.8 %all-to-all-start.1 = ((f32[32,512,64]{1,2,0:T(8,128)}), f32[32,512,64]{1,2,0:T(8,128)}, u32[]{:S(2)}, u32[]{:S(2)}) async-start(f32[32,512,64]{1,2,0:T(8,128)} %bitcast.89), calls=%async_computation.1 | async-start | bytes 8388608 | tf_op jit(solution)/shard_map/all_to_all | solution.py:109
  540.7 115.2 %all-to-all-start.3 = ((f32[16,128,512]{1,0,2:T(8,128)}), f32[16,128,512]{1,0,2:T(8,128)}, u32[]{:S(2)}, u32[]{:S(2)}) async-start(f32[16,128,512]{1,0,2:T(8,128)} %copy.72), calls=%async_computation.3 | async-start | bytes 8388608 | tf_op jit(solution)/shard_map/all_to_all | solution.py:117
  547.7 4.3 copy-start.5
  648.7 5.4 copy-start.6
where the time goes:
time: 678 us; the launch traced here: 667 us
  blocking collectives  199 us (29%)
  local copies, waits for them, and re-layouts  189 us (28%)
  other arithmetic  116 us (17%)
  waiting for transfers between devices  89.8 us (13%)
  matrix products  57.8 us (9%)
  starting transfers between devices  13.6 us (2%)
    unnamed x1, blocking collectives  96.5 us
    reduce_sum x16, other arithmetic, pair_value(): return jnp.sum(cutoff * table_rows, axis=-1).reshape(2, tile_cells)  95.3 us
    all_to_all x1, waiting for transfers between devices, on_device(): lax.all_to_all(lax.all_to_all(z_first, 'gx', split_axis=0, concat_axis=1,...  89.8 us
    all_to_all x1, blocking collectives, on_device(): lax.all_to_all(z_first, 'gx', split_axis=0, concat_axis=1, tiled=True)  51.9 us
    all_to_all x1, blocking collectives, on_device(): lax.all_to_all(smoothed_pencil, 'gx', split_axis=1, concat_axis=0, tiled=...  50.7 us
    reshape x2, local copies, waits for them, and re-layouts, evaluate(): return values.reshape(tile_count, tile_cells)  37.2 us
    reshape x2, local copies, waits for them, and re-layouts, on_device(): log_crit.reshape(blocks_x, tile_edge, blocks_y, tile_edge, blocks_z, tile...  25.6 us
    another operation x1, local copies, waits for them, and re-layouts, evaluate(): field_rows.reshape(tile_count // 2, 2, tile_cells)  16.7 us
  transfers between devices with their start and end apart: 2, of which 1 were waited for; matrix products, arithmetic and copies ran while one was open for 2% of the time, Pallas kernels for 0%

commit v1 on v0

v1 whole, which is shorter than its diff:
```python
import functools
import math

import jax
import jax.numpy as jnp
from jax import lax
from jax.experimental import pallas as pl
from jax.experimental.pallas import tpu as pltpu
from jax.sharding import PartitionSpec as P

steepness = 3.0
vmem_grant = 60 * 1024 * 1024
MESH = pl.DeviceIdType.MESH


def node_growth(nodes):
    return [math.exp(steepness * (-2.5 + 5.0 * q / (nodes - 1))) for q in range(nodes // 2, nodes)]


def join(left, right):
    num_left, den_left = left
    num_right, den_right = right
    return (num_left * den_right + num_right * den_left, den_left * den_right)


def integral(field, upper, lower, growth, scratch_a, scratch_b):
    pairs = len(growth)
    v = jnp.exp(field * steepness)
    y = v + jnp.exp(field * -steepness)
    scratch_a[...] = upper + lower
    position = lax.broadcasted_iota(jnp.int32, upper.shape, 0).astype(jnp.float32)
    step = math.log(growth[1] / growth[0])
    rise = jnp.exp(position * step + math.log(growth[0]))
    fall = jnp.exp(position * -step - math.log(growth[0]))
    scratch_b[...] = upper * fall + lower * rise
    total = None
    for first in range(0, pairs, 4):
        terms = []
        for p in range(first, min(first + 4, pairs)):
            num = scratch_a[pl.ds(p, 1), :] * v + scratch_b[pl.ds(p, 1), :]
            terms.append((num, y + (growth[p] + 1.0 / growth[p])))
        while len(terms) > 1:
            terms = [
                join(terms[i], terms[i + 1]) if i + 1 < len(terms) else terms[i]
                for i in range(0, len(terms), 2)
            ]
        part = terms[0][0] * (1.0 / terms[0][1])
        total = part if total is None else total + part
    return total


def eval_kernel(
    growth, tiles, field_ref, bins_ref, live_ref, table_ref, recomb_ref, zfirst_ref, sums_ref,
    turned, values, scratch_a, scratch_b,
):
    cells_x, rows, depth_all = field_ref.shape
    edge = depth_all // tiles
    pairs = len(growth)
    bins_total = table_ref.shape[1]
    for row in range(rows):
        turned[row] = field_ref[:, row, :].T

    def step(i, carry):
        row, tile = i // tiles, i % tiles
        span = pl.ds(pl.multiple_of(tile * edge, edge), edge)
        levels = lax.broadcasted_iota(jnp.int32, (bins_total, cells_x), 0)
        onehot = jnp.where(levels == bins_ref[pl.ds(i, 1), :], 1.0, 0.0).astype(jnp.bfloat16)
        rows_here = jnp.dot(table_ref[...], onehot, preferred_element_type=jnp.float32)
        rows_here = rows_here * live_ref[pl.ds(i, 1), :]
        out = integral(
            turned[row, span, :], rows_here[:pairs], rows_here[pairs:], growth, scratch_a, scratch_b
        )
        values[row, span, :] = out
        sums_ref[pl.ds(i, 1), :] = jnp.sum(out, axis=0, keepdims=True)
        return carry

    lax.fori_loop(0, rows * tiles, step, 0)
    for row in range(rows):
        recomb_ref[:, row, :] = values[row].T
        zfirst_ref[:, row, :] = values[row]


def evaluate(log_crit, bins, live, table, growth, tiles):
    cells_x, cells_y, depth_all = log_crit.shape
    rows = 8
    nodes, bins_total = table.shape
    return pl.pallas_call(
        functools.partial(eval_kernel, growth, tiles),
        grid=(cells_y // rows,),
        in_specs=[
            pl.BlockSpec((cells_x, rows, depth_all), lambda j: (0, j, 0)),
            pl.BlockSpec((rows * tiles, cells_x), lambda j: (j, 0)),
            pl.BlockSpec((rows * tiles, cells_x), lambda j: (j, 0)),
            pl.BlockSpec((nodes, bins_total), lambda j: (0, 0)),
        ],
        out_specs=[
            pl.BlockSpec((cells_x, rows, depth_all), lambda j: (0, j, 0)),
            pl.BlockSpec((depth_all, rows, cells_x), lambda j: (0, j, 0)),
            pl.BlockSpec((rows * tiles, cells_x), lambda j: (j, 0)),
        ],
        out_shape=[
            jax.ShapeDtypeStruct((cells_x, cells_y, depth_all), jnp.float32),
            jax.ShapeDtypeStruct((depth_all, cells_y, cells_x), jnp.float32),
            jax.ShapeDtypeStruct((cells_y * tiles, cells_x), jnp.float32),
        ],
        scratch_shapes=[
            pltpu.VMEM((rows, depth_all, cells_x), jnp.float32),
            pltpu.VMEM((rows, depth_all, cells_x), jnp.float32),
            pltpu.VMEM((nodes // 2, cells_x), jnp.float32),
            pltpu.VMEM((nodes // 2, cells_x), jnp.float32),
        ],
        compiler_params=pltpu.CompilerParams(vmem_limit_bytes=vmem_grant),
        name="evaluate",
    )(log_crit, bins, live, table)


def halves(value):
    high = value.astype(jnp.bfloat16)
    return high, (value - high.astype(jnp.float32)).astype(jnp.bfloat16)


def outer_halves(value):
    high = lax.reduce_precision(value, 8, 7)
    low = lax.reduce_precision(value - high, 8, 7)
    return high.astype(jnp.bfloat16), low.astype(jnp.bfloat16)


def dot3(a_high, a_low, b_high, b_low):
    dot = functools.partial(jnp.dot, preferred_element_type=jnp.float32)
    return dot(a_high, b_high) + (dot(a_high, b_low) + dot(a_low, b_high))


def smooth_kernel(
    span_x, span_y, zfirst, cy_high, cy_low, cx_high, cx_low, out,
    plane, done, high, low, send_sem, recv_sem, own_sem, back_send, back_recv, back_own,
):
    planes, devices, cells_y, cells_x = zfirst.shape
    size_y, size_x = high.shape
    block = 128 if size_y % 128 == 0 else size_y
    gx, gy = lax.axis_index("gx"), lax.axis_index("gy")
    me = gx * span_y + gy

    def at(i, j):
        return {"gx": i, "gy": j}

    def place(ref, k, i, j):
        return ref.at[
            k,
            pl.ds(pl.multiple_of(j * cells_y, cells_y), cells_y),
            pl.ds(pl.multiple_of(i * cells_x, cells_x), cells_x),
        ]

    def each_peer(act):
        def body(n, carry):
            offset_y, offset_x = n // span_x, n % span_x
            act(lax.rem(gx + offset_x, span_x), lax.rem(gy + offset_y, span_y))
            return carry

        lax.fori_loop(1, devices, body, 0)

    barrier = pltpu.get_barrier_semaphore()
    each_peer(
        lambda i, j: pl.semaphore_signal(barrier, inc=1, device_id=at(i, j), device_id_type=MESH)
    )
    for k in range(planes):
        pltpu.make_async_copy(zfirst.at[k, me], place(plane, k, gx, gy), own_sem.at[k]).start()
    pl.semaphore_wait(barrier, devices - 1)

    def send_plane(k):
        def act(i, j):
            pltpu.make_async_remote_copy(
                src_ref=zfirst.at[k, i * span_y + j],
                dst_ref=place(plane, k, gx, gy),
                send_sem=send_sem.at[k],
                recv_sem=recv_sem.at[k],
                device_id=at(i, j),
                device_id_type=MESH,
            ).start()

        each_peer(act)

    def send_back(k):
        def act(i, j):
            pltpu.make_async_remote_copy(
                src_ref=place(done, k, i, j),
                dst_ref=out.at[k, me],
                send_sem=back_send.at[k],
                recv_sem=back_recv.at[k],
                device_id=at(i, j),
                device_id_type=MESH,
            ).start()

        each_peer(act)
        pltpu.make_async_copy(place(done, k, gx, gy), out.at[k, me], back_own.at[k]).start()

    def wait_others(sem, k):
        some = zfirst.at[0, pl.ds(0, devices - 1)]
        pltpu.make_async_copy(some, some, sem.at[k]).wait()

    def wait_own(sem, k):
        one = zfirst.at[0, 0]
        pltpu.make_async_copy(one, one, sem.at[k]).wait()

    for k in range(planes):
        send_plane(k)

    def finish_plane(k, carry):
        wait_own(own_sem, k)
        wait_others(recv_sem, k)

        def split(r, carry):
            rows = pl.ds(pl.multiple_of(r * block, block), block)
            high[rows, :], low[rows, :] = halves(plane[k, rows, :])
            return carry

        lax.fori_loop(0, size_y // block, split, 0)

        def multiply(r, carry):
            rows = pl.ds(pl.multiple_of(r * block, block), block)
            along_y = dot3(cy_high[rows, :], cy_low[rows, :], high[...], low[...])
            y_high, y_low = halves(along_y)
            done[k, rows, :] = dot3(y_high, y_low, cx_high[...], cx_low[...])
            return carry

        lax.fori_loop(0, size_y // block, multiply, 0)
        send_back(k)
        return carry

    lax.fori_loop(0, planes, finish_plane, 0)
    for k in range(planes):
        wait_others(send_sem, k)
        wait_others(back_send, k)
        wait_own(back_own, k)
        wait_others(back_recv, k)


def smooth(zfirst, cy, cx, span_x, span_y):
    planes, devices, cells_y, cells_x = zfirst.shape
    size_y, size_x = cy.shape[0], cx.shape[0]
    anywhere = pl.BlockSpec(memory_space=pl.ANY)
    inside = pl.BlockSpec(memory_space=pltpu.VMEM)
    sems = pltpu.SemaphoreType.DMA((planes,))
    return pl.pallas_call(
        functools.partial(smooth_kernel, span_x, span_y),
        in_specs=[anywhere] + [inside] * 4,
        out_specs=anywhere,
        out_shape=jax.ShapeDtypeStruct(zfirst.shape, jnp.float32),
        scratch_shapes=[
            pltpu.VMEM((planes, size_y, size_x), jnp.float32),
            pltpu.VMEM((planes, size_y, size_x), jnp.float32),
            pltpu.VMEM((size_y, size_x), jnp.bfloat16),
            pltpu.VMEM((size_y, size_x), jnp.bfloat16),
        ]
        + [sems] * 6,
        compiler_params=pltpu.CompilerParams(
            collective_id=0, has_side_effects=True, vmem_limit_bytes=vmem_grant
        ),
        name="smooth",
    )(zfirst, *outer_halves(cy), *outer_halves(cx))


def turn_kernel(source_ref, out_ref):
    for row in range(source_ref.shape[1]):
        out_ref[:, row, :] = source_ref[:, row, :].T


def turn(source):
    depth_all, cells_y, cells_x = source.shape
    rows = 8
    return pl.pallas_call(
        turn_kernel,
        grid=(cells_y // rows,),
        in_specs=[pl.BlockSpec((depth_all, rows, cells_x), lambda j: (0, j, 0))],
        out_specs=pl.BlockSpec((cells_x, rows, depth_all), lambda j: (0, j, 0)),
        out_shape=jax.ShapeDtypeStruct((cells_x, cells_y, depth_all), jnp.float32),
        name="turn",
    )(source)


def circulant(gain):
    length = gain.shape[0]
    half = length // 2
    indices = jnp.arange(length, dtype=jnp.int32)
    freq = jnp.concatenate(
        [jnp.arange(half + 1, dtype=jnp.int32), jnp.arange(1, half, dtype=jnp.int32)]
    )
    angles = (
        2.0 * math.pi / length * (indices[:, None] * freq[None, :] % length).astype(jnp.float32)
    )
    table = jnp.where(indices[None, :] < half + 1, jnp.cos(angles), jnp.sin(angles))
    weight = jnp.concatenate([gain[: half + 1], gain[1:half]])
    doubled = jnp.where((freq == 0) | (freq == half), 1.0, 2.0).astype(jnp.float32)
    return jnp.dot(
        table * (weight * doubled / length), table.T, precision=lax.Precision.HIGHEST
    )


def on_device(log_crit, col_bins, rate_table, tile_mask, tile_route, filt_x, filt_y):
    blocks_x, blocks_y, tiles = tile_mask.shape
    cells_x, cells_y, depth_all = log_crit.shape
    edge = cells_x // blocks_x
    span_x, span_y = lax.axis_size("gx"), lax.axis_size("gy")
    devices = span_x * span_y
    nodes = rate_table.shape[1]
    half = nodes // 2

    bins = col_bins.transpose(1, 2, 0).reshape(cells_y * tiles, cells_x)
    live = (tile_mask == 1).astype(jnp.float32).transpose(1, 2, 0)
    live = jnp.broadcast_to(
        live[:, None, :, :, None], (blocks_y, edge, tiles, blocks_x, edge)
    ).reshape(cells_y * tiles, cells_x)
    table = jnp.concatenate([rate_table[:, half:], rate_table[:, half - 1 :: -1]], axis=1).T

    recomb, zfirst, sums = evaluate(log_crit, bins, live, table, node_growth(nodes), tiles)

    tile_means = jnp.sum(
        sums.reshape(blocks_y, edge, tiles, blocks_x, edge), axis=(1, 4)
    ) / (edge * edge * edge)
    route = tile_route.transpose(1, 2, 0)
    capacity = blocks_x * blocks_y * tiles // 2
    route_ids = jnp.arange(span_y, dtype=jnp.int32)
    contribution = (
        jnp.sum(
            jnp.where(route[..., None] == route_ids, tile_means[..., None], 0.0), axis=(0, 1, 2)
        )
        / capacity
    )
    device_load = lax.psum_scatter(contribution, "gy", scatter_dimension=0, tiled=True)[0]

    back = smooth(
        zfirst.reshape(depth_all // devices, devices, cells_y, cells_x),
        circulant(filt_y), circulant(filt_x), span_x, span_y,
    )
    smoothed = turn(back.reshape(depth_all, cells_y, cells_x))
    return (recomb, smoothed, device_load.reshape(1, 1))


def solution(mesh):
    placed = (
        P("gx", "gy", None),
        P("gx", "gy", None),
        P(),
        P("gx", "gy", None),
        P("gx", "gy", None),
        P(),
        P(),
    )
    return jax.shard_map(
        on_device,
        mesh=mesh,
        in_specs=placed,
        out_specs=(P("gx", "gy", None), P("gx", "gy", None), P("gx", "gy")),
        check_vma=False,
    )
```

time: 678 us -> 326 us (0.48)
  Pallas kernels: 0 us -> 272 us
  local copies, waits for them, and re-layouts: 189 us -> 4.87 us
  blocking collectives: 199 us -> 19.4 us
  other arithmetic: 116 us -> 2.44 us
  waiting for transfers between devices: 89.8 us -> 0 us
  matrix products: 57.8 us -> 22.6 us
  starting transfers between devices: 13.6 us -> 0 us
    pallas_call x0 -> x3, Pallas kernels: none -> 272 us  [the longest x1 187 us: smooth(): pl.pallas_call(functools.partial(smooth_kernel, span_x, span_y), in_specs...]
    all_to_all x2 -> x0, blocking collectives: 103 us -> none  [the longest x1 51.9 us: on_device(): lax.all_to_all(z_first, 'gx', split_axis=0, concat_axis=1, tiled=True)]
    reduce_sum x18 -> x2, other arithmetic: 99.5 us -> 0.3 us  [the longest x1 0.2 us: on_device(): jnp.sum(sums.reshape(blocks_y, edge, tiles, blocks_x, edge), axis=(1, 4))]
    all_to_all x2 -> x0, waiting for transfers between devices: 89.8 us -> none  [the longest x1 89.8 us: on_device(): lax.all_to_all(lax.all_to_all(z_first, 'gx', split_axis=0, concat_axis=1,...]
    unnamed x1, blocking collectives: 96.5 us -> 19.4 us
    reshape x7 -> x2, local copies, waits for them, and re-layouts: 76.8 us -> 1.15 us  [the longest x1 0.89 us: on_device(): live = jnp.broadcast_to(live[:, None, :, :, None], (blocks_y, edge, tiles...]
    dot_general x20 -> x2, matrix products: 57.8 us -> 22.6 us  [circulant(): jnp.dot(table * (weight * doubled / length), table.T, precision=lax.Preci...]
    all_to_all x6 -> x0, local copies, waits for them, and re-layouts: 20.4 us -> none  [the longest x3 9.5 us: on_device(): lax.all_to_all(smoothed_pencil, 'gx', split_axis=1, concat_axis=0, tiled=...]
  transfers between devices with their start and end apart: 2 -> 0, of which waited for: 1 -> 0; matrix products, arithmetic and copies ran while one was open for 2% -> 0% of each run, Pallas kernels for 0% -> 0%
where the time goes in v1:
time: 326 us; the launch traced here: 322 us
  Pallas kernels  272 us (83%)
  matrix products  22.6 us (7%)
  blocking collectives  19.4 us (6%)
  local copies, waits for them, and re-layouts  4.87 us (1%)
    pallas_call x1, Pallas kernels, smooth(): pl.pallas_call(functools.partial(smooth_kernel, span_x, span_y), in_specs...  187 us
    pallas_call x1, Pallas kernels, evaluate(): pl.pallas_call(functools.partial(eval_kernel, growth, tiles), grid=(cells...  76.4 us
    dot_general x2, matrix products, circulant(): jnp.dot(table * (weight * doubled / length), table.T, precision=lax.Preci...  22.6 us
    unnamed x1, blocking collectives  19.4 us
    pallas_call x1, Pallas kernels, turn(): pl.pallas_call(turn_kernel, grid=(cells_y // rows,), in_specs=[pl.BlockSp...  8.5 us

profile of v1, /device:TPU:8, one launch (start us, length us, event | category | flops | bytes accessed | tf_op | source)
XLA Modules:
  0.0 321.7 jit_solution(14104998146030577540)
XLA Ops:
  0.6 0.8 slice.23
  1.4 0.8 fusion.18
  2.2 0.8 slice.21
  2.9 0.8 fusion.17
  3.7 11.2 %fusion.5 = (bf16[512,512]{1,0:T(8,128)(2,1)}, bf16[512,512]{1,0:T(8,128)(2,1)}) fusion(s32[512]{0:T(512)S(1)} %get-tuple-element.11, pred[512]{0:T(512)(128)(4,1)S(1)} %iota_compare_fusion.1, f32[512]{0:T(512)S(1)} %fusion.17), kind=kOutput, calls=%fused_computation.12 | convolution fusion | flops 1620049920 | bytes 1053184 | tf_op jit(solution)/shard_map/dot_general | solution.py:293
  14.9 0.0 copy-start.1
  14.9 0.0 copy-start.2
  14.9 11.4 %fusion.7 = (bf16[512,512]{1,0:T(8,128)(2,1)}, bf16[512,512]{1,0:T(8,128)(2,1)}) fusion(s32[512]{0:T(512)S(1)} %get-tuple-element.11, pred[512]{0:T(512)(128)(4,1)S(1)} %iota_compare_fusion.1, f32[512]{0:T(512)S(1)} %get-tuple-element.9), kind=kOutput, calls=%fused_computation.14 | convolution fusion | flops 1620049920 | bytes 1053184 | tf_op jit(solution)/shard_map/dot_general | solution.py:293
  26.3 0.0 copy-done.1
  26.3 0.6 maximum_bitcast_fusion.table_ref
  26.9 0.0 copy-done.2
  26.9 0.1 copy.14
  27.0 0.1 broadcast_in_dim.50
  27.2 0.9 reshape.98.live_ref
  28.1 76.4 %evaluate.1 = (f32[128,64,128]{2,1,0:T(8,128)}, f32[128,64,128]{2,1,0:T(8,128)}, f32[256,128]{1,0:T(8,128)}) custom-call(f32[128,64,128]{2,1,0:T(8,128)} %field_ref.1, s32[256,128]{1,0:T(8,128)} %bitcast.16, f32[256,128]{1,0:T(8,128)} %reshape.98.live_ref, bf16[64,128]{1,0:T(8,128)(2,1)} %maximum_bitcast_fusion.table_ref), custom_call_target="tpu_custom_call" | custom-call | tf_op jit(solution)/shard_map/evaluate/pallas_call | solution.py:87
  104.4 186.9 %smooth.1 = f32[4,32,64,128]{3,2,1,0:T(8,128)} custom-call(f32[4,32,64,128]{3,2,1,0:T(8,128)} %bitcast.15, bf16[512,512]{1,0:T(8,128)(2,1)} %get-tuple-element.15.cy_high, bf16[512,512]{1,0:T(8,128)(2,1)} %get-tuple-element.14.cy_low, bf16[512,512]{1,0:T(8,128)(2,1)} %get-tuple-element.13.cx_high, bf16[512,512]{1,0:T(8,128)(2,1)} %get-tuple-element.12.cx_low), custom_call_target="tpu_custom_call" | custom-call | tf_op jit(solution)/shard_map/smooth/pallas_call | solution.py:243
  291.3 0.0 copy-start
  291.3 0.0 copy-start.3
  291.3 0.0 copy-start.4
  291.3 8.5 %turn.1 = f32[128,64,128]{2,1,0:T(8,128)} custom-call(f32[128,64,128]{2,1,0:T(8,128)} %bitcast.14), custom_call_target="tpu_custom_call" | custom-call | tf_op jit(solution)/shard_map/turn/pallas_call | solution.py:270
  299.8 0.0 copy-done
  299.8 0.3 reshape.101
  300.1 0.2 reduce_sum.18
  300.3 0.0 copy-done.3
  300.3 0.1 copy.15
  300.4 0.1 select_reduce_fusion
  300.5 19.4 %all-reduce = f32[8]{0:T(128)S(1)} all-reduce(f32[8]{0:T(128)S(1)} %broadcast_multiply_fusion.1), channel_id=2, replica_groups=mesh['gx'=4,'gy'=8] {'gy'}, use_global_device_ids=true, to_apply=%region_2.3.clone | all-reduce | flops 8 | bytes 64
  319.9 0.0 copy-done.4
  319.9 0.6 dynamic-slice
  320.5 1.2 dynamic-slice.1
  (8 shorter events, 0.1 us)
Async XLA Ops:
  14.9 11.4 %copy-start.1 = (bf16[128,64]{0,1:T(8,128)(2,1)S(1)}, bf16[128,64]{0,1:T(8,128)(2,1)}, u32[]{:S(2)}) copy-start(bf16[128,64]{0,1:T(8,128)(2,1)} %param.9) | copy-start | bytes 49156
  14.9 12.0 %copy-start.2 = (s32[4,2,4]{2,1,0:T(2,128)S(1)}, s32[4,2,4]{2,1,0:T(2,128)}, u32[]{:S(2)}) copy-start(s32[4,2,4]{2,1,0:T(2,128)} %param.10) | copy-start | bytes 388
  291.3 8.5 %copy-start = (f32[256,128]{1,0:T(8,128)S(1)}, f32[256,128]{1,0:T(8,128)}, u32[]{:S(2)}) copy-start(f32[256,128]{1,0:T(8,128)} %get-tuple-element.8) | copy-start | bytes 393220
  291.3 9.0 %copy-start.3 = (s32[4,2,4]{2,1,0:T(2,128)S(1)}, s32[4,2,4]{2,1,0:T(2,128)}, u32[]{:S(2)}) copy-start(s32[4,2,4]{2,1,0:T(2,128)} %param.11) | copy-start | bytes 388
  291.3 28.6 %copy-start.4 = (u32[32]{0:T(128)S(1)}, u32[32]{0:T(128)}, u32[]{:S(2)}) copy-start(u32[32]{0:T(128)} %constant.48) | copy-start | bytes 388

commit v2 on v1

--- a/solution.py
+++ b/solution.py
@@ -23,21 +23,15 @@
     return (num_left * den_right + num_right * den_left, den_left * den_right)
 
 
-def integral(field, upper, lower, growth, scratch_a, scratch_b):
+def integral(field, i, growth, coef_a, coef_b):
     pairs = len(growth)
     v = jnp.exp(field * steepness)
     y = v + jnp.exp(field * -steepness)
-    scratch_a[...] = upper + lower
-    position = lax.broadcasted_iota(jnp.int32, upper.shape, 0).astype(jnp.float32)
-    step = math.log(growth[1] / growth[0])
-    rise = jnp.exp(position * step + math.log(growth[0]))
-    fall = jnp.exp(position * -step - math.log(growth[0]))
-    scratch_b[...] = upper * fall + lower * rise
     total = None
     for first in range(0, pairs, 4):
         terms = []
         for p in range(first, min(first + 4, pairs)):
-            num = scratch_a[pl.ds(p, 1), :] * v + scratch_b[pl.ds(p, 1), :]
+            num = coef_a[i, pl.ds(p, 1), :] * v + coef_b[i, pl.ds(p, 1), :]
             terms.append((num, y + (growth[p] + 1.0 / growth[p])))
         while len(terms) > 1:
             terms = [
@@ -50,8 +44,8 @@
 
 
 def eval_kernel(
-    growth, tiles, field_ref, bins_ref, live_ref, table_ref, recomb_ref, zfirst_ref, sums_ref,
-    turned, values, scratch_a, scratch_b,
+    growth, tiles, field_ref, bins_ref, live_ref, table_ref, rise_ref, recomb_ref, zfirst_ref,
+    sums_ref, turned, values, coef_a, coef_b,
 ):
     cells_x, rows, depth_all = field_ref.shape
     edge = depth_all // tiles
@@ -60,20 +54,25 @@
     for row in range(rows):
         turned[row] = field_ref[:, row, :].T
 
-    def step(i, carry):
-        row, tile = i // tiles, i % tiles
-        span = pl.ds(pl.multiple_of(tile * edge, edge), edge)
+    def gather(i, carry):
         levels = lax.broadcasted_iota(jnp.int32, (bins_total, cells_x), 0)
         onehot = jnp.where(levels == bins_ref[pl.ds(i, 1), :], 1.0, 0.0).astype(jnp.bfloat16)
         rows_here = jnp.dot(table_ref[...], onehot, preferred_element_type=jnp.float32)
         rows_here = rows_here * live_ref[pl.ds(i, 1), :]
-        out = integral(
-            turned[row, span, :], rows_here[:pairs], rows_here[pairs:], growth, scratch_a, scratch_b
-        )
+        upper, lower = rows_here[:pairs], rows_here[pairs:]
+        coef_a[i] = upper + lower
+        coef_b[i] = upper * rise_ref[1] + lower * rise_ref[0]
+        return carry
+
+    def step(i, carry):
+        row, tile = i // tiles, i % tiles
+        span = pl.ds(pl.multiple_of(tile * edge, edge), edge)
+        out = integral(turned[row, span, :], i, growth, coef_a, coef_b)
         values[row, span, :] = out
         sums_ref[pl.ds(i, 1), :] = jnp.sum(out, axis=0, keepdims=True)
         return carry
 
+    lax.fori_loop(0, rows * tiles, gather, 0, unroll=8)
     lax.fori_loop(0, rows * tiles, step, 0)
     for row in range(rows):
         recomb_ref[:, row, :] = values[row].T
@@ -84,6 +83,8 @@
     cells_x, cells_y, depth_all = log_crit.shape
     rows = 8
     nodes, bins_total = table.shape
+    ends = jnp.array([growth, [1.0 / e for e in growth]], jnp.float32)
+    rise = jnp.broadcast_to(ends[:, :, None], (2, nodes // 2, cells_x))
     return pl.pallas_call(
         functools.partial(eval_kernel, growth, tiles),
         grid=(cells_y // rows,),
@@ -92,6 +93,7 @@
             pl.BlockSpec((rows * tiles, cells_x), lambda j: (j, 0)),
             pl.BlockSpec((rows * tiles, cells_x), lambda j: (j, 0)),
             pl.BlockSpec((nodes, bins_total), lambda j: (0, 0)),
+            pl.BlockSpec((2, nodes // 2, cells_x), lambda j: (0, 0, 0)),
         ],
         out_specs=[
             pl.BlockSpec((cells_x, rows, depth_all), lambda j: (0, j, 0)),
@@ -106,12 +108,12 @@
         scratch_shapes=[
             pltpu.VMEM((rows, depth_all, cells_x), jnp.float32),
             pltpu.VMEM((rows, depth_all, cells_x), jnp.float32),
-            pltpu.VMEM((nodes // 2, cells_x), jnp.float32),
-            pltpu.VMEM((nodes // 2, cells_x), jnp.float32),
+            pltpu.VMEM((rows * tiles, nodes // 2, cells_x), jnp.float32),
+            pltpu.VMEM((rows * tiles, nodes // 2, cells_x), jnp.float32),
         ],
         compiler_params=pltpu.CompilerParams(vmem_limit_bytes=vmem_grant),
         name="evaluate",
-    )(log_crit, bins, live, table)
+    )(log_crit, bins, live, table, rise)
 
 
 def halves(value):
@@ -131,8 +133,9 @@
 
 
 def smooth_kernel(
-    span_x, span_y, zfirst, cy_high, cy_low, cx_high, cx_low, out,
+    span_x, span_y, zfirst, loads, cy_high, cy_low, cx_high, cx_low, out, load_parts,
     plane, done, high, low, send_sem, recv_sem, own_sem, back_send, back_recv, back_own,
+    load_sems,
 ):
     planes, devices, cells_y, cells_x = zfirst.shape
     size_y, size_x = high.shape
@@ -201,6 +204,22 @@
         one = zfirst.at[0, 0]
         pltpu.make_async_copy(one, one, sem.at[k]).wait()
 
+    own_load = pltpu.make_async_copy(loads.at[gy], load_parts.at[gy], load_sems.at[2])
+    own_load.start()
+
+    def send_load(n, carry):
+        j = lax.rem(gy + n, span_y)
+        pltpu.make_async_remote_copy(
+            src_ref=loads.at[j],
+            dst_ref=load_parts.at[gy],
+            send_sem=load_sems.at[0],
+            recv_sem=load_sems.at[1],
+            device_id=at(gx, j),
+            device_id_type=MESH,
+        ).start()
+        return carry
+
+    lax.fori_loop(1, span_y, send_load, 0)
     for k in range(planes):
         send_plane(k)
 
@@ -227,6 +246,10 @@
         return carry
 
     lax.fori_loop(0, planes, finish_plane, 0)
+    some_loads = loads.at[pl.ds(0, span_y - 1)]
+    pltpu.make_async_copy(some_loads, some_loads, load_sems.at[0]).wait()
+    pltpu.make_async_copy(some_loads, some_loads, load_sems.at[1]).wait()
+    own_load.wait()
     for k in range(planes):
         wait_others(send_sem, k)
         wait_others(back_send, k)
@@ -234,7 +257,7 @@
         wait_others(back_recv, k)
 
 
-def smooth(zfirst, cy, cx, span_x, span_y):
+def smooth(zfirst, loads, cy, cx, span_x, span_y):
     planes, devices, cells_y, cells_x = zfirst.shape
     size_y, size_x = cy.shape[0], cx.shape[0]
     anywhere = pl.BlockSpec(memory_space=pl.ANY)
@@ -242,21 +265,25 @@
     sems = pltpu.SemaphoreType.DMA((planes,))
     return pl.pallas_call(
         functools.partial(smooth_kernel, span_x, span_y),
-        in_specs=[anywhere] + [inside] * 4,
-        out_specs=anywhere,
-        out_shape=jax.ShapeDtypeStruct(zfirst.shape, jnp.float32),
+        in_specs=[anywhere] * 2 + [inside] * 4,
+        out_specs=[anywhere] * 2,
+        out_shape=[
+            jax.ShapeDtypeStruct(zfirst.shape, jnp.float32),
+            jax.ShapeDtypeStruct(loads.shape, jnp.float32),
+        ],
         scratch_shapes=[
             pltpu.VMEM((planes, size_y, size_x), jnp.float32),
             pltpu.VMEM((planes, size_y, size_x), jnp.float32),
             pltpu.VMEM((size_y, size_x), jnp.bfloat16),
             pltpu.VMEM((size_y, size_x), jnp.bfloat16),
         ]
-        + [sems] * 6,
+        + [sems] * 6
+        + [pltpu.SemaphoreType.DMA((3,))],
         compiler_params=pltpu.CompilerParams(
             collective_id=0, has_side_effects=True, vmem_limit_bytes=vmem_grant
         ),
         name="smooth",
-    )(zfirst, *outer_halves(cy), *outer_halves(cx))
+    )(zfirst, loads, *outer_halves(cy), *outer_halves(cx))
 
 
 def turn_kernel(source_ref, out_ref):
@@ -277,21 +304,31 @@
     )(source)
 
 
-def circulant(gain):
+def wave_freq(length):
+    half = length // 2
+    return jnp.concatenate(
+        [jnp.arange(half + 1, dtype=jnp.int32), jnp.arange(1, half, dtype=jnp.int32)]
+    )
+
+
+def wave_table(length):
+    half = length // 2
+    indices = jnp.arange(length, dtype=jnp.int32)
+    turns = indices[:, None] * wave_freq(length)[None, :] % length
+    angles = 2.0 * math.pi / length * turns.astype(jnp.float32)
+    shift = jnp.where(indices < half + 1, 0.0, math.pi / 2)[None, :]
+    return lax.optimization_barrier(jnp.cos(angles - shift))
+
+
+def circulant(gain, table):
     length = gain.shape[0]
     half = length // 2
-    indices = jnp.arange(length, dtype=jnp.int32)
-    freq = jnp.concatenate(
-        [jnp.arange(half + 1, dtype=jnp.int32), jnp.arange(1, half, dtype=jnp.int32)]
-    )
-    angles = (
-        2.0 * math.pi / length * (indices[:, None] * freq[None, :] % length).astype(jnp.float32)
-    )
-    table = jnp.where(indices[None, :] < half + 1, jnp.cos(angles), jnp.sin(angles))
+    freq = wave_freq(length)
     weight = jnp.concatenate([gain[: half + 1], gain[1:half]])
     doubled = jnp.where((freq == 0) | (freq == half), 1.0, 2.0).astype(jnp.float32)
-    return jnp.dot(
-        table * (weight * doubled / length), table.T, precision=lax.Precision.HIGHEST
+    scaled = lax.optimization_barrier(table * (weight * doubled / length))
+    return lax.dot_general(
+        scaled, table, (((1,), (1,)), ((), ())), precision=lax.Precision.HIGHEST
     )
 
 
@@ -325,12 +362,14 @@
         )
         / capacity
     )
-    device_load = lax.psum_scatter(contribution, "gy", scatter_dimension=0, tiled=True)[0]
-
-    back = smooth(
+    table_x = wave_table(filt_x.shape[0])
+    table_y = table_x if filt_y.shape == filt_x.shape else wave_table(filt_y.shape[0])
+    back, load_parts = smooth(
         zfirst.reshape(depth_all // devices, devices, cells_y, cells_x),
-        circulant(filt_y), circulant(filt_x), span_x, span_y,
-    )
+        jnp.broadcast_to(contribution[:, None, None], (span_y, 8, 128)),
+        circulant(filt_y, table_y), circulant(filt_x, table_x), span_x, span_y,
+    )
+    device_load = jnp.sum(load_parts[:, 0, 0])
     smoothed = turn(back.reshape(depth_all, cells_y, cells_x))
     return (recomb, smoothed, device_load.reshape(1, 1))
 

time: 326 us -> 273 us (0.84)
  Pallas kernels: 272 us -> 249 us
  blocking collectives: 19.4 us -> 0 us
  matrix products: 22.6 us -> 5.73 us
  other arithmetic: 2.44 us -> 8.6 us
    pallas_call x1, Pallas kernels: 76.4 us -> 53.4 us  [evaluate(): pl.pallas_call(functools.partial(eval_kernel, growth, tiles), grid=(cells...]
    unnamed x1 -> x0, blocking collectives: 19.4 us -> none
    dot_general x2, matrix products: 22.6 us -> 5.73 us  [circulant(): lax.dot_general(scaled, table, (((1,), (1,)), ((), ())), precision=lax.Pr...]
    cos x0 -> x1, other arithmetic: none -> 3.82 us  [wave_table(): return lax.optimization_barrier(jnp.cos(angles - shift))]
where the time goes in v2:
time: 273 us; the launch traced here: 271 us
  Pallas kernels  249 us (91%)
  other arithmetic  8.6 us (3%)
  local copies, waits for them, and re-layouts  6.68 us (2%)
  matrix products  5.73 us (2%)
    pallas_call x1, Pallas kernels, smooth(): pl.pallas_call(functools.partial(smooth_kernel, span_x, span_y), in_specs...  188 us
    pallas_call x1, Pallas kernels, evaluate(): pl.pallas_call(functools.partial(eval_kernel, growth, tiles), grid=(cells...  53.4 us
    pallas_call x1, Pallas kernels, turn(): pl.pallas_call(turn_kernel, grid=(cells_y // rows,), in_specs=[pl.BlockSp...  8.44 us
    dot_general x2, matrix products, circulant(): lax.dot_general(scaled, table, (((1,), (1,)), ((), ())), precision=lax.Pr...  5.73 us

profile of v2, /device:TPU:8, one launch (start us, length us, event | category | flops | bytes accessed | tf_op | source)
XLA Modules:
  0.0 271.1 jit_solution(2257193807016664856)
XLA Ops:
  0.6 0.8 slice.26
  1.4 0.8 slice.24
  2.1 0.8 fusion.14
  2.9 0.8 fusion.13
  3.7 0.7 fusion.12
  4.4 0.1 copy.13
  4.5 0.8 copy.14
  5.2 0.7 fusion.16
  6.0 0.6 maximum_bitcast_fusion.table_ref
  6.6 0.1 broadcast_in_dim.54
  6.7 0.9 reshape.105.live_ref
  7.6 3.8 %fusion.8 = f32[512,512]{1,0:T(8,128)S(1)} fusion(f32[512]{0:T(512)S(1)} %get-tuple-element.24, s32[512]{0:T(512)S(1)} %get-tuple-element.15), kind=kLoop, calls=%fused_computation.15 | loop fusion | flops 3932160 | bytes 1052672 | tf_op jit(solution)/shard_map/cos | solution.py:320
  11.4 0.0 copy-start
  11.4 0.3 broadcast_multiply_fusion
  11.7 2.9 %fusion.1 = (bf16[512,512]{1,0:T(8,128)(2,1)}, bf16[512,512]{1,0:T(8,128)(2,1)}) fusion(f32[512,512]{1,0:T(8,128)S(1)} %get-tuple-element.19, f32[512,512]{1,0:T(8,128)S(1)} %fusion.8), kind=kOutput, calls=%fused_computation.8 | convolution fusion | flops 1611923456 | bytes 3145728 | tf_op jit(solution)/shard_map/dot_general | solution.py:330
  14.6 2.9 %fusion.3 = (bf16[512,512]{1,0:T(8,128)(2,1)}, bf16[512,512]{1,0:T(8,128)(2,1)}) fusion(f32[512,512]{1,0:T(8,128)S(1)} %get-tuple-element.18, f32[512,512]{1,0:T(8,128)S(1)} %fusion.8), kind=kOutput, calls=%fused_computation.10 | convolution fusion | flops 1611923456 | bytes 3145728 | tf_op jit(solution)/shard_map/dot_general | solution.py:330
  17.5 0.0 copy-done
  17.5 0.7 broadcast_in_dim.55.rise_ref
  18.1 53.4 %evaluate.1 = (f32[128,64,128]{2,1,0:T(8,128)}, f32[128,64,128]{2,1,0:T(8,128)}, f32[256,128]{1,0:T(8,128)}) custom-call(f32[128,64,128]{2,1,0:T(8,128)} %field_ref.1, s32[256,128]{1,0:T(8,128)} %bitcast.19, f32[256,128]{1,0:T(8,128)} %reshape.105.live_ref, bf16[64,128]{1,0:T(8,128)(2,1)} %maximum_bitcast_fusion.table_ref, ...), custom_call_target="tpu_custom_call" | custom-call | tf_op jit(solution)/shard_map/evaluate/pallas_call | solution.py:88
  71.5 1.2 reshape.107
  72.7 0.2 reduce_sum.27
  72.9 0.1 select_reduce_fusion
  73.0 0.7 broadcast_in_dim.58.loads
  73.7 187.6 %smooth.1 = (f32[4,32,64,128]{3,2,1,0:T(8,128)}, f32[8,8,128]{2,1,0:T(8,128)}) custom-call(f32[4,32,64,128]{3,2,1,0:T(8,128)} %bitcast.17, f32[8,8,128]{2,1,0:T(8,128)} %broadcast_in_dim.58.loads, bf16[512,512]{1,0:T(8,128)(2,1)} %get-tuple-element.21.cy_high, bf16[512,512]{1,0:T(8,128)(2,1)} %get-tuple-element.20.cy_low, ...), custom_call_target="tpu_custom_call" | custom-call | tf_op jit(solution)/shard_map/smooth/pallas_call | solution.py:266
  261.3 1.4 slice_reduce_fusion
  262.7 8.4 %turn.1 = f32[128,64,128]{2,1,0:T(8,128)} custom-call(f32[128,64,128]{2,1,0:T(8,128)} %bitcast.18), custom_call_target="tpu_custom_call" | custom-call | tf_op jit(solution)/shard_map/turn/pallas_call | solution.py:297
  (5 shorter events, 0.0 us)
Async XLA Ops:
  11.4 6.0 %copy-start = (f32[2,32]{1,0:T(2,128)S(1)}, f32[2,32]{1,0:T(2,128)}, u32[]{:S(2)}) copy-start(f32[2,32]{1,0:T(2,128)} %constant.45.clone) | copy-start | bytes 772
